TPU v7x, 32 devices: a whole 2x2x4 slice. The times are simulated.
32 devices in a mesh: row: 4 (over z), col: 8 (over y, x, core).
Axes of the slice: x: 2, y: 2, z: 4, core: 2. Of those that a mesh axis runs over, the one named last changes fastest.
Arguments:
- a_matrix: float32 [16384, 16384], P('row', 'col'), may hold values from -2.25 to 2.25
- b_matrix: float32 [16384, 16384], P('row', 'col'), may hold values from -0.1 to 3.1
- x_block: float32 [16384, 64], P('row'), may hold values from -6 to 6
- r_block: float32 [16384, 64], P('row'), may hold values from -6 to 6
- p_block: float32 [16384, 64], P('row'), may hold values from -6 to 6
Outputs:
- x_next: float32 [16384, 64], P('row')
- r_next: float32 [16384, 64], P('row')
- p_next: float32 [16384, 64], P('row')
All inputs are finite; a program needn't handle non-finite values.
Results may differ from a plain program's by a relative error of at most 0.0003.
Values sent between devices are 32-bit elements; how exact they have to be, the bound alone decides.
A program may use at most 192 MiB of HBM per device.

v0:
```python
import functools
import math

import jax
import jax.numpy as jnp
from jax import lax
from jax.experimental import pallas as pl
from jax.experimental.pallas import tpu as pltpu
from jax.sharding import PartitionSpec as P

NS_STEPS = 8
HIGHEST = lax.Precision.HIGHEST
HIGH = lax.Precision.HIGH


def mm(left, right, lc=1, rc=0, precision=HIGHEST):
    return lax.dot_general(
        left, right, (((lc,), (rc,)), ((), ())), precision=precision, preferred_element_type=jnp.float32
    )


def total(value):
    return lax.psum(lax.psum(value, "row"), "col")


def spread_t(value_t, tile_cols):
    ratio = lax.axis_size("col") // lax.axis_size("row")
    col_index = lax.axis_index("col")
    part = lax.dynamic_slice_in_dim(value_t, col_index % ratio * tile_cols, tile_cols, 1)
    kept = jnp.where(lax.axis_index("row") == col_index // ratio, part, 0.0)
    return lax.psum(kept, "row")


def block_inverse(block):
    size = block.shape[0]
    rows = lax.broadcasted_iota(jnp.int32, (size, size), 0)
    cols = lax.broadcasted_iota(jnp.int32, (size, size), 1)
    inverse = jnp.where(rows == cols, 1.0, 0.0)
    for j in range(size):
        pivot = 1.0 / block[j : j + 1, j : j + 1]
        factor = jnp.where(rows[:, :1] > j, block[:, j : j + 1], 0.0)
        inverse = inverse - factor * (inverse[j : j + 1] * pivot)
        block = block - factor * (block[j : j + 1] * pivot)
    diag = jnp.sum(jnp.where(rows == cols, block, 0.0), axis=1, keepdims=True)
    return inverse / jnp.sqrt(diag)


def ritz_kernel(order, ga_ref, gb_ref, w_ref, ch_ref, wa_ref, wb_ref, linv_ref, sym_ref):
    n, k = w_ref.shape[0], ch_ref.shape[1]
    gb = gb_ref[...]
    sym_ref[...] = 0.5 * (gb + gb.T)
    ga = ga_ref[...]
    ga = 0.5 * (ga + ga.T)
    nb = n // k
    cut = lambda ref, i, j: ref[i * k : (i + 1) * k, j * k : (j + 1) * k]
    linv_ref[...] = jnp.zeros((n, n), jnp.float32)
    low, inv = {}, {}
    for j in range(nb):
        for i in range(j, nb):
            rest = cut(sym_ref, i, j)
            for m in range(j):
                rest = rest - mm(low[i, m], low[j, m], 1, 1)
            if i == j:
                inv[j, j] = block_inverse(rest)
            else:
                low[i, j] = mm(rest, inv[j, j], 1, 1)
    for j in range(nb):
        for i in range(j + 1, nb):
            total = mm(low[i, j], inv[j, j])
            for m in range(j + 1, i):
                total = total + mm(low[i, m], inv[m, j])
            inv[i, j] = -mm(inv[i, i], total)
    for (i, j), value in inv.items():
        linv_ref[i * k : (i + 1) * k, j * k : (j + 1) * k] = value
    linv = linv_ref[...]
    linv_t = linv.T
    middle = mm(mm(linv, ga), linv_t)
    middle = 0.5 * (middle + middle.T)
    rows = lax.broadcasted_iota(jnp.int32, (n, n), 0)
    cols = lax.broadcasted_iota(jnp.int32, (n, n), 1)
    ident = jnp.where(rows == cols, 1.0, 0.0)
    shift = jnp.sum(middle * ident) / n
    centred = middle - shift * ident
    sign_est = centred / jnp.sqrt(jnp.full((1, 1), jnp.sum(centred * centred) + 1e-06))
    for turn in range(NS_STEPS):
        sign_est = 1.5 * sign_est - 0.5 * mm(sign_est, mm(sign_est, sign_est))
    filtered = (0.5 * (ident - sign_est))[:, :k]
    coords = mm(linv_t, filtered) * math.sqrt(order)
    reduced = mm(filtered.T, mm(middle, filtered))
    ch_ref[...] = mm(coords, reduced)
    w_ref[:, :k] = coords
    w_ref[:, k:] = jnp.where(lax.broadcasted_iota(jnp.int32, (n, k), 0) >= k, coords, 0.0)
    w = w_ref[...]
    w_t = w.T
    wa_ref[...] = mm(w_t, mm(ga, w))
    wb_ref[...] = mm(w_t, mm(sym_ref[...], w))


def ritz(order, width, gram_a, gram_b):
    n, k = gram_a.shape[0], width
    shape = lambda *dims: jax.ShapeDtypeStruct(dims, jnp.float32)
    return pl.pallas_call(
        functools.partial(ritz_kernel, order),
        out_shape=(shape(n, 2 * k), shape(n, k), shape(2 * k, 2 * k), shape(2 * k, 2 * k)),
        in_specs=[pl.BlockSpec(memory_space=pltpu.VMEM)] * 2,
        out_specs=[pl.BlockSpec(memory_space=pltpu.VMEM)] * 4,
        scratch_shapes=[pltpu.VMEM((n, n), jnp.float32)] * 2,
        name="ritz",
    )(gram_a, gram_b)


def extend(kept, fresh):
    k = fresh.shape[1]
    x, r, p = fresh[:k], fresh[k : 2 * k], fresh[2 * k :]
    return jnp.concatenate(
        [
            jnp.concatenate([kept[:k, :k], x, kept[:k, k:]], axis=1),
            jnp.concatenate([x.T, r, p.T], axis=1),
            jnp.concatenate([kept[k:, :k], p, kept[k:, k:]], axis=1),
        ],
        axis=0,
    )


def local(order, a_matrix, b_matrix, x_block, r_block, p_block):
    tile_cols = a_matrix.shape[1]
    k = x_block.shape[1]
    panel = jnp.concatenate([x_block, r_block, p_block], axis=1)
    matched_t = spread_t(panel.T, tile_cols)
    prod_a = mm(a_matrix, matched_t, 1, 1, HIGH)
    prod_b = mm(b_matrix, matched_t, 1, 1, HIGH)
    grams = total(jnp.concatenate([mm(panel, prod_a, 0, 0), mm(panel, prod_b, 0, 0)], axis=1))
    w, ch, kept_a, kept_b = ritz(order, k, grams[:, : 3 * k], grams[:, 3 * k :])
    coords = w[:, :k]
    resid_t = lax.psum(mm(coords, prod_a, 0, 1) - mm(ch, prod_b, 0, 1), "col")
    matched_t = spread_t(resid_t, tile_cols)
    both = mm(panel, w)
    panel = jnp.concatenate([both[:, :k], resid_t.T, both[:, k:]], axis=1)
    fresh_a = mm(a_matrix, matched_t, 1, 1, HIGH)
    fresh_b = mm(b_matrix, matched_t, 1, 1, HIGH)
    grams = total(jnp.concatenate([mm(panel, fresh_a, 0, 0), mm(panel, fresh_b, 0, 0)], axis=1))
    w2, ch2, _, _ = ritz(order, k, extend(kept_a, grams[:, :k]), extend(kept_b, grams[:, k:]))
    c2 = w2[:, :k]
    outer = lambda c: jnp.concatenate([c[:k], c[2 * k :]], axis=0)
    on_a, on_b = mm(w, outer(c2)), mm(w, outer(ch2))
    resid_t = lax.psum(
        (mm(on_a, prod_a, 0, 1) + mm(c2[k : 2 * k], fresh_a, 0, 1))
        - (mm(on_b, prod_b, 0, 1) + mm(ch2[k : 2 * k], fresh_b, 0, 1)),
        "col",
    )
    both = mm(panel, w2)
    return (both[:, :k], resid_t.T, both[:, k:])


def solution(mesh):
    def whole(a_matrix, b_matrix, x_block, r_block, p_block):
        return jax.shard_map(
            functools.partial(local, a_matrix.shape[0]),
            mesh=mesh,
            in_specs=(P("row", "col"), P("row", "col"), P("row", None), P("row", None), P("row", None)),
            out_specs=(P("row", None), P("row", None), P("row", None)),
            check_vma=False,
        )(a_matrix, b_matrix, x_block, r_block, p_block)

    return whole
```

profile of v0, /device:TPU:13, one launch (start us, length us, event | category | flops | bytes accessed | tf_op | source)
XLA Modules:
  0.0 629.3 jit_solution(8663134355446850811)
XLA Ops:
  7.2 1.3 constant_dynamic-update-slice_fusion.2
  8.6 1.3 constant_dynamic-update-slice_fusion.1
  9.9 1.3 constant_dynamic-update-slice_fusion
  11.2 1.5 select_bitcast_fusion
  13.3 68.5 %all-reduce.9.cloned.1.call-done = f32[192,2048]{1,0:T(8,128)} async-done(((f32[192,2048]{1,0:T(8,128)}), f32[192,2048]{1,0:T(8,128)}) %all-reduce.9.cloned.1.call-update) | async-done | bytes 1572880 | tf_op jit(solution)/shard_map/psum | solution.py:31
  81.8 20.8 %fusion.32 = f32[192,4096]{1,0:T(8,128)S(1)} fusion(f32[192,2048]{1,0:T(8,128)} %all-reduce.9.cloned.1.call-done, f32[4096,2048]{1,0:T(8,128)} %param.5), kind=kOutput, calls=%fused_computation.49 | convolution fusion | flops 9663676416 | bytes 38273024 | tf_op jit(solution)/shard_map/dot_general | solution.py:17
  102.6 4.6 fusion.33
  107.2 22.2 %fusion.34 = f32[192,4096]{1,0:T(8,128)} fusion(f32[192,2048]{1,0:T(8,128)} %all-reduce.9.cloned.1.call-done, f32[4096,2048]{1,0:T(8,128)} %param.6), kind=kOutput, calls=%fused_computation.51 | convolution fusion | flops 9663676416 | bytes 38273024 | tf_op jit(solution)/shard_map/dot_general | solution.py:17
  129.4 5.5 fusion.35
  134.9 0.8 pad_maximum_fusion.4
  135.8 34.0 %all-reduce.11.cloned.1.call-done = f32[192,384]{1,0:T(8,128)} async-done(((f32[192,384]{1,0:T(8,128)}), f32[192,384]{1,0:T(8,128)}) %all-reduce.11.cloned.1.call-update) | async-done | bytes 294928 | tf_op jit(solution)/shard_map/psum | solution.py:23
  169.9 57.5 %all-reduce.13.cloned.1.call-done = f32[192,384]{1,0:T(8,128)} async-done(((f32[192,384]{1,0:T(8,128)}), f32[192,384]{1,0:T(8,128)}) %all-reduce.13.cloned.1.call-update) | async-done | bytes 294928 | tf_op jit(solution)/shard_map/psum | solution.py:23
  227.4 1.8 fusion.24
  229.2 29.4 %ritz.2 = (f32[192,128]{1,0:T(8,128)}, f32[192,64]{1,0:T(8,128)}, f32[128,128]{1,0:T(8,128)}, f32[128,128]{1,0:T(8,128)}) custom-call(f32[192,192]{1,0:T(8,128)} %get-tuple-element.20.ga_ref, f32[192,192]{1,0:T(8,128)} %get-tuple-element.19.gb_ref), custom_call_target="tpu_custom_call" | custom-call | tf_op jit(solution)/shard_map/ritz/pallas_call | solution.py:102
  258.6 3.3 fusion.5
  262.0 3.1 convolution_subtract_fusion
  265.1 5.5 fusion.36
  270.6 50.5 %all-reduce.15.cloned.1.call-done = f32[64,4096]{1,0:T(8,128)} async-done(((f32[64,4096]{1,0:T(8,128)}), f32[64,4096]{1,0:T(8,128)}) %all-reduce.15.cloned.1.call-update) | async-done | bytes 1048592 | tf_op jit(solution)/shard_map/psum | solution.py:135
  321.2 1.9 dynamic-slice_select_fusion
  323.1 3.1 fusion.23
  326.3 0.7 fusion.29
  327.0 34.8 %all-reduce.17.cloned.1.call-done = f32[64,2048]{1,0:T(8,128)} async-done(((f32[64,2048]{1,0:T(8,128)}), f32[64,2048]{1,0:T(8,128)}) %all-reduce.17.cloned.1.call-update) | async-done | bytes 524304 | tf_op jit(solution)/shard_map/psum | solution.py:31
  361.8 22.1 %fusion.37 = f32[64,4096]{1,0:T(8,128)} fusion(f32[64,2048]{1,0:T(8,128)} %all-reduce.17.cloned.1.call-done, f32[4096,2048]{1,0:T(8,128)} %param.5), kind=kOutput, calls=%fused_computation.54 | convolution fusion | flops 3221225472 | bytes 35127296 | tf_op jit(solution)/shard_map/dot_general | solution.py:17
  383.9 5.3 fusion.4
  389.2 22.3 %fusion.38 = f32[64,4096]{1,0:T(8,128)} fusion(f32[64,2048]{1,0:T(8,128)} %all-reduce.17.cloned.1.call-done, f32[4096,2048]{1,0:T(8,128)} %param.6), kind=kOutput, calls=%fused_computation.55 | convolution fusion | flops 3221225472 | bytes 35127296 | tf_op jit(solution)/shard_map/dot_general | solution.py:17
  411.4 5.3 fusion.3
  418.1 33.7 %all-reduce.19.cloned.1.call-done = f32[192,128]{0,1:T(8,128)} async-done(((f32[192,128]{0,1:T(8,128)}), f32[192,128]{0,1:T(8,128)}) %all-reduce.19.cloned.1.call-update) | async-done | bytes 98320 | tf_op jit(solution)/shard_map/psum | solution.py:23
  452.3 0.7 fusion.31
  453.0 55.4 %all-reduce.21.cloned.1.call-done = f32[192,128]{0,1:T(8,128)} async-done(((f32[192,128]{0,1:T(8,128)}), f32[192,128]{0,1:T(8,128)}) %all-reduce.21.cloned.1.call-update) | async-done | bytes 98320 | tf_op jit(solution)/shard_map/psum | solution.py:23
  508.5 1.5 fusion.25
  510.2 0.8 pad_maximum_fusion.6
  511.0 0.7 copy.17
  512.4 0.8 copy.20
  513.2 0.9 pad_maximum_fusion.8
  514.2 1.4 copy.9
  515.7 1.0 maximum_maximum_fusion
  516.6 0.8 copy.19.ga_ref
  517.4 1.7 maximum_maximum_fusion.1.gb_ref
  519.1 29.6 %ritz.3 = (f32[192,128]{1,0:T(8,128)}, f32[192,64]{1,0:T(8,128)}, f32[128,128]{1,0:T(8,128)}, f32[128,128]{1,0:T(8,128)}) custom-call(f32[192,192]{1,0:T(8,128)} %copy.19.ga_ref, f32[192,192]{1,0:T(8,128)} %maximum_maximum_fusion.1.gb_ref), custom_call_target="tpu_custom_call" | custom-call | tf_op jit(solution)/shard_map/ritz/pallas_call | solution.py:102
  548.7 0.9 fusion.27
  549.6 5.6 fusion.2
  555.5 2.1 fusion.40
  557.9 2.1 fusion.39
  560.0 1.8 convolution_add_fusion.1
  561.8 2.1 fusion.1
  564.0 1.5 fusion.22
  565.5 54.5 %all-reduce.23.cloned.1.call-done = f32[4096,64]{0,1:T(8,128)} async-done(((f32[4096,64]{0,1:T(8,128)}), f32[4096,64]{0,1:T(8,128)}) %all-reduce.23.cloned.1.call-update) | async-done | bytes 1048592 | tf_op jit(solution)/shard_map/psum | solution.py:146
  620.0 2.3 copy.32
  (53 shorter events, 4.3 us)
Async XLA Ops:
  7.2 74.6 %all-reduce.9.cloned.1.call-start = ((), (), s32[]{:S(2)}) async-start(), calls=%async_computation | async-start | bytes 3145728 | tf_op jit(solution)/shard_map/psum | solution.py:31
  11.2 2.1 copy-start.2
  12.7 157.2 %all-reduce.11.cloned.1.call-start = ((), (), s32[]{:S(2)}) async-start(), calls=%async_computation.1 | async-start | bytes 589824 | tf_op jit(solution)/shard_map/psum | solution.py:23
  135.8 91.6 %all-reduce.13.cloned.1.call-start = ((), (), s32[]{:S(2)}) async-start(), calls=%async_computation.2 | async-start | bytes 589824 | tf_op jit(solution)/shard_map/psum | solution.py:23
  169.9 151.3 %all-reduce.15.cloned.1.call-start = ((), (), s32[]{:S(2)}) async-start(), calls=%async_computation.3 | async-start | bytes 2097152 | tf_op jit(solution)/shard_map/psum | solution.py:135
  258.6 3.3 copy-start
  258.6 3.3 copy-start.12
  261.9 3.2 copy-start.6
  265.1 96.7 %all-reduce.17.cloned.1.call-start = ((), (), s32[]{:S(2)}) async-start(), calls=%async_computation.4 | async-start | bytes 1048576 | tf_op jit(solution)/shard_map/psum | solution.py:31
  270.6 55.5 %copy-start.10 = (f32[128,128]{1,0:T(8,128)S(1)}, f32[128,128]{1,0:T(8,128)}, u32[]{:S(2)}) copy-start(f32[128,128]{1,0:T(8,128)} %get-tuple-element.12) | copy-start | bytes 196612
  270.6 55.6 %copy-start.9 = (f32[128,128]{1,0:T(8,128)S(1)}, f32[128,128]{1,0:T(8,128)}, u32[]{:S(2)}) copy-start(f32[128,128]{1,0:T(8,128)} %get-tuple-element.11) | copy-start | bytes 196612
  323.1 128.8 %all-reduce.19.cloned.1.call-start = ((), (), s32[]{:S(2)}) async-start(), calls=%async_computation.5 | async-start | bytes 262144 | tf_op jit(solution)/shard_map/psum | solution.py:23
  417.4 91.1 %all-reduce.21.cloned.1.call-start = ((), (), s32[]{:S(2)}) async-start(), calls=%async_computation.6 | async-start | bytes 262144 | tf_op jit(solution)/shard_map/psum | solution.py:23
  451.9 168.1 %all-reduce.23.cloned.1.call-start = ((), (), s32[]{:S(2)}) async-start(), calls=%async_computation.7 | async-start | bytes 2097152 | tf_op jit(solution)/shard_map/psum | solution.py:146
  510.1 3.2 copy-start.7
  513.2 2.4 copy-start.8
  548.7 6.5 %copy-start.11 = (f32[192,64]{1,0:T(8,128)S(1)}, f32[192,64]{1,0:T(8,128)}, u32[]{:S(2)}) copy-start(f32[192,64]{1,0:T(8,128)} %get-tuple-element.14) | copy-start | bytes 147460
  548.7 6.8 %copy-start.1 = (f32[192,4096]{1,0:T(8,128)S(1)}, f32[192,4096]{1,0:T(8,128)}, u32[]{:S(2)}) copy-start(f32[192,4096]{1,0:T(8,128)} %fusion.34) | copy-start | bytes 9437188
  557.6 2.4 copy-start.3
  557.8 4.0 copy-start.4
  561.8 2.1 copy-start.5
Sparse Core Ops, SparseCore 0:
  12.8 68.9 all-reduce.8
  135.9 33.9 all-reduce.10
  172.9 54.3 all-reduce.12
  265.2 55.9 all-reduce.14
  323.9 37.8 all-reduce.16
  417.5 34.2 all-reduce.18
  454.9 53.5 all-reduce.20
  564.1 55.8 all-reduce.22
where the time goes:
time: 641 us; the launch traced here: 629 us
  waiting for transfers between devices  389 us (61%)
  matrix products  134 us (21%)
  Pallas kernels  59 us (9%)
  local copies, waits for them, and re-layouts  22.6 us (4%)
  between operations  14.6 us (2%)
  other arithmetic  9.16 us (1%)
    psum x4, waiting for transfers between devices, total(): return lax.psum(lax.psum(value, 'row'), 'col')  181 us
    dot_general x18, matrix products, mm(): lax.dot_general(left, right, (((lc,), (rc,)), ((), ())), precision=precis...  134 us
    psum x2, waiting for transfers between devices, spread_t(): return lax.psum(kept, 'row')  103 us
    pallas_call x2, Pallas kernels, ritz(): pl.pallas_call(functools.partial(ritz_kernel, order), out_shape=(shape(n,...  59 us
    psum x1, waiting for transfers between devices, local(): lax.psum(mm(on_a, prod_a, 0, 1) + mm(c2[k:2 * k], fresh_a, 0, 1) - (mm(on...  54.5 us
    psum x1, waiting for transfers between devices, local(): resid_t = lax.psum(mm(coords, prod_a, 0, 1) - mm(ch, prod_b, 0, 1), 'col')  50.5 us
  transfers between devices with their start and end apart: 8, of which 8 were waited for; matrix products, arithmetic and copies ran while one was open for 2% of the time, Pallas kernels for 0%

commit v1 on v0

--- a/solution.py
+++ b/solution.py
@@ -19,16 +19,441 @@
     )
 
 
-def total(value):
-    return lax.psum(lax.psum(value, "row"), "col")
-
-
-def spread_t(value_t, tile_cols):
-    ratio = lax.axis_size("col") // lax.axis_size("row")
-    col_index = lax.axis_index("col")
-    part = lax.dynamic_slice_in_dim(value_t, col_index % ratio * tile_cols, tile_cols, 1)
-    kept = jnp.where(lax.axis_index("row") == col_index // ratio, part, 0.0)
-    return lax.psum(kept, "row")
+MESH = pl.DeviceIdType.MESH
+
+
+def remote(src, dst, send_sem, recv_sem, **where):
+    return pltpu.make_async_remote_copy(
+        src_ref=src, dst_ref=dst, send_sem=send_sem, recv_sem=recv_sem, device_id=where, device_id_type=MESH
+    )
+
+
+def greet(barrier, **where):
+    pl.semaphore_signal(barrier, inc=1, device_id=where, device_id_type=MESH)
+
+
+def meet(n_rows, others):
+    r = lax.axis_index("row")
+    barrier = pltpu.get_barrier_semaphore()
+    has_up, has_down = r < n_rows - 1, r > 0
+
+    @pl.when(has_up)
+    def _():
+        greet(barrier, row=r + 1)
+
+    @pl.when(has_down)
+    def _():
+        greet(barrier, row=r - 1)
+
+    @pl.when(has_up & has_down)
+    def _():
+        pl.semaphore_wait(barrier, others + 2)
+
+    @pl.when(jnp.logical_not(has_up & has_down))
+    def _():
+        pl.semaphore_wait(barrier, others + 1)
+
+
+def halves(value):
+    high = value.astype(jnp.bfloat16)
+    return high, (value - high.astype(jnp.float32)).astype(jnp.bfloat16)
+
+
+def dot(left, right, lc=1, rc=0):
+    return lax.dot_general(left, right, (((lc,), (rc,)), ((), ())), preferred_element_type=jnp.float32)
+
+
+def apply_kernel(
+    n_rows, n_cols, chunks, x_ref, a_ref, b_ref, on_a_ref, on_b_ref, tile_ref, x_parts, tile, up_sems, down_sems, recv_sems
+):
+    n, k = pl.program_id(0), pl.program_id(1)
+    depth = pl.num_programs(1)
+    now = n * depth + k
+    steps = chunks
+    m, tk = x_ref.shape[0], a_ref.shape[0]
+    r, c = lax.axis_index("row"), lax.axis_index("col")
+    ratio = n_cols // n_rows
+    home, part = c // ratio, c % ratio
+    width = tile.shape[1]
+    step = width // chunks
+    has_up, has_down = r < n_rows - 1, r > 0
+
+    def slot(i):
+        return tile.at[:, pl.ds(pl.multiple_of(i * step, 128), step)]
+
+    def up(i, src):
+        return remote(src, slot(i), up_sems.at[i], recv_sems.at[i], row=r + 1)
+
+    def down(i, src):
+        return remote(src, slot(i), down_sems.at[i], recv_sems.at[i], row=r - 1)
+
+    def relay(i):
+        @pl.when(r > home)
+        def _():
+            down(i, slot(i)).wait_recv()
+
+            @pl.when(has_up)
+            def _():
+                up(i, slot(i)).start()
+
+        @pl.when(r < home)
+        def _():
+            up(i, slot(i)).wait_recv()
+
+            @pl.when(has_down)
+            def _():
+                down(i, slot(i)).start()
+
+    @pl.when(now == 0)
+    def _():
+        meet(n_rows, 0)
+
+        @pl.when(r == home)
+        def _():
+            for i in range(chunks):
+                own = x_ref.at[:, pl.ds(pl.multiple_of(part * width + i * step, 128), step)]
+
+                @pl.when(has_up)
+                def _():
+                    up(i, own).start()
+
+                @pl.when(has_down)
+                def _():
+                    down(i, own).start()
+
+        high, low = halves(x_ref[...])
+        x_parts[:m] = high
+        x_parts[m:] = low
+
+    for mat_ref, out_ref in ((a_ref, on_a_ref), (b_ref, on_b_ref)):
+        high, low = halves(mat_ref[...])
+        x = x_parts[:, pl.ds(pl.multiple_of(k * tk, 128), tk)]
+        both = dot(x, high)
+        value = both[:m] + (both[m:] + dot(x[:m], low))
+
+        @pl.when(k == 0)
+        def _():
+            out_ref[...] = value
+
+        @pl.when(k > 0)
+        def _():
+            out_ref[...] += value
+
+    for away in range(1, n_rows):
+        lag = 2 * away
+
+        @pl.when(((r == home + away) | (r == home - away)) & (now >= lag) & (now < chunks + lag))
+        def _():
+            relay(now - lag)
+
+    @pl.when(now == steps - 1)
+    def _():
+        for away in range(1, n_rows):
+
+            @pl.when((r == home + away) | (r == home - away))
+            def _():
+                for i in range(max(steps - 2 * away, 0), chunks):
+                    relay(i)
+
+        @pl.when((r >= home) & has_up)
+        def _():
+            for i in range(chunks):
+                up(i, slot(i)).wait_send()
+
+        @pl.when((r <= home) & has_down)
+        def _():
+            for i in range(chunks):
+                down(i, slot(i)).wait_send()
+
+        @pl.when(r == home)
+        def _():
+            tile_ref[...] = x_ref[:, pl.ds(pl.multiple_of(part * width, 128), width)]
+
+        @pl.when(r != home)
+        def _():
+            tile_ref[...] = tile[...]
+
+
+def apply_both(x_rows, a_matrix, b_matrix, collective_id):
+    n_rows, n_cols = lax.axis_size("row"), lax.axis_size("col")
+    m, rows = x_rows.shape
+    cols = a_matrix.shape[1]
+    tk, tn = min(1024, rows), min(512, cols)
+    grid = (cols // tn, rows // tk)
+    chunks = grid[0] * grid[1]
+    block = pl.BlockSpec((tk, tn), lambda n, k: (k, n))
+    out = pl.BlockSpec((m, tn), lambda n, k: (0, n))
+    shape = jax.ShapeDtypeStruct((m, cols), jnp.float32)
+    return pl.pallas_call(
+        functools.partial(apply_kernel, n_rows, n_cols, chunks),
+        out_shape=(shape,) * 3,
+        grid=grid,
+        in_specs=[pl.BlockSpec(memory_space=pltpu.VMEM), block, block],
+        out_specs=[out, out, pl.BlockSpec(memory_space=pltpu.VMEM)],
+        scratch_shapes=[pltpu.VMEM((2 * m, rows), jnp.bfloat16), pltpu.VMEM((m, cols), jnp.float32)]
+        + [pltpu.SemaphoreType.DMA((chunks,))] * 3,
+        compiler_params=pltpu.CompilerParams(
+            collective_id=collective_id, has_side_effects=True, dimension_semantics=("arbitrary", "arbitrary")
+        ),
+        name="apply_both",
+    )(x_rows, a_matrix, b_matrix)
+
+
+LAG = 3
+
+
+def gather_kernel(n_rows, n_cols, chunks, x_ref, o_ref, from_up, from_down, inward, row_send, up_recv, down_recv, send, recv):
+    r, c = lax.axis_index("row"), lax.axis_index("col")
+    ratio = n_cols // n_rows
+    home, part = c // ratio, c % ratio
+    width = x_ref.shape[1]
+    step = width // chunks
+    bits = n_cols.bit_length() - 1
+    has_up, has_down = r < n_rows - 1, r > 0
+
+    def bit(value, i):
+        return value // 2**i % 2
+
+    def flip(i):
+        return c + 2**i * (1 - 2 * bit(c, i))
+
+    barrier = pltpu.get_barrier_semaphore()
+    for i in range(bits):
+        greet(barrier, col=flip(i))
+    meet(n_rows, bits)
+
+    def lanes(ref, k):
+        return ref.at[:, k * step : (k + 1) * step]
+
+    def to_down(k, src):
+        return remote(src, lanes(from_up, k), row_send.at[k], up_recv.at[k], row=r - 1)
+
+    def to_up(k, src):
+        return remote(src, lanes(from_down, k), row_send.at[k], down_recv.at[k], row=r + 1)
+
+    def reduce(k):
+        own = lanes(x_ref, k)
+
+        @pl.when(r > home)
+        def _():
+            @pl.when(has_up)
+            def _():
+                to_down(k, own).wait_recv()
+                lanes(inward, k)[...] = own[...] + lanes(from_up, k)[...]
+                to_down(k, lanes(inward, k)).start()
+
+            @pl.when(jnp.logical_not(has_up))
+            def _():
+                to_down(k, own).start()
+
+        @pl.when(r < home)
+        def _():
+            @pl.when(has_down)
+            def _():
+                to_up(k, own).wait_recv()
+                lanes(inward, k)[...] = own[...] + lanes(from_down, k)[...]
+                to_up(k, lanes(inward, k)).start()
+
+            @pl.when(jnp.logical_not(has_down))
+            def _():
+                to_up(k, own).start()
+
+        @pl.when(r == home)
+        def _():
+            mine = o_ref.at[:, pl.ds(pl.multiple_of(part * width + k * step, 128), step)]
+
+            @pl.when(has_up)
+            def _():
+                to_down(k, own).wait_recv()
+
+            @pl.when(has_down)
+            def _():
+                to_up(k, own).wait_recv()
+
+            @pl.when(has_up & has_down)
+            def _():
+                mine[...] = own[...] + (lanes(from_up, k)[...] + lanes(from_down, k)[...])
+
+            @pl.when(jnp.logical_not(has_down))
+            def _():
+                mine[...] = own[...] + lanes(from_up, k)[...]
+
+            @pl.when(jnp.logical_not(has_up))
+            def _():
+                mine[...] = own[...] + lanes(from_down, k)[...]
+
+    def copies(p, k):
+        apart = [(bit(c, i) + bit(r * ratio + p, i)) % 2 for i in range(bits)]
+        top = [*range(bits - 1, 0, -1)]
+        turn = k % len(top)
+        order = [*top[turn:], *top[:turn], 0]
+        spot = o_ref.at[:, p * width + k * step : p * width + (k + 1) * step]
+        out = []
+        for j, i in enumerate(order):
+            later = sum(apart[x] for x in order[j:])
+            out.append((later == 0, remote(spot, spot, send.at[p, k, j], recv.at[p, k], col=flip(i))))
+        return out, sum(apart) > 0
+
+    def broadcast(p, k, root):
+        sends, inner = copies(p, k)
+
+        @pl.when(jnp.logical_not(inner) if root else inner)
+        def _():
+            if not root:
+                sends[0][1].wait_recv()
+            for j, (condition, copy) in enumerate(sends):
+                if root:
+                    copy.start()
+                elif j:
+
+                    @pl.when(condition)
+                    def _():
+                        copy.start()
+
+    for i in range(chunks + LAG):
+        if i < chunks:
+            reduce(i)
+            for p in range(ratio):
+                broadcast(p, i, True)
+        if i >= LAG:
+            for p in range(ratio):
+                broadcast(p, i - LAG, False)
+    for k in range(chunks):
+        @pl.when(r > home)
+        def _():
+            to_down(k, lanes(x_ref, k)).wait_send()
+
+        @pl.when(r < home)
+        def _():
+            to_up(k, lanes(x_ref, k)).wait_send()
+
+        for p in range(ratio):
+            for condition, copy in copies(p, k)[0]:
+
+                @pl.when(condition)
+                def _():
+                    copy.wait_send()
+
+
+def gather_sum(value, collective_id):
+    n_rows, n_cols = lax.axis_size("row"), lax.axis_size("col")
+    m, width = value.shape
+    ratio = n_cols // n_rows
+    chunks = min(8, width // 128)
+    dma = pltpu.SemaphoreType.DMA
+    return pl.pallas_call(
+        functools.partial(gather_kernel, n_rows, n_cols, chunks),
+        out_shape=jax.ShapeDtypeStruct((m, ratio * width), jnp.float32),
+        in_specs=[pl.BlockSpec(memory_space=pltpu.VMEM)],
+        out_specs=pl.BlockSpec(memory_space=pltpu.VMEM),
+        scratch_shapes=[pltpu.VMEM((m, width), jnp.float32)] * 3
+        + [dma((chunks,))] * 3
+        + [dma((ratio, chunks, n_cols.bit_length() - 1)), dma((ratio, chunks))],
+        compiler_params=pltpu.CompilerParams(collective_id=collective_id, has_side_effects=True),
+        name="gather_sum",
+    )(value)
+
+
+def sum_kernel(n_rows, n_cols, over_rows, x_ref, o_ref, pair_buf, part, group_buf, row_buf, *sems):
+    pair_send, pair_recv, group_send, group_recv, row_send, row_recv, all_send, all_recv, back_send, back_recv = sems
+    r, c = lax.axis_index("row"), lax.axis_index("col")
+    half = n_cols // 2
+    g, h = c // 2, c % 2
+    partner = 2 * g + 1 - h
+    flat = len(x_ref.shape) == 2
+    step = x_ref.shape[-1] // n_cols
+
+    def piece(ref, index):
+        return ref.at[:, pl.ds(pl.multiple_of(index * step, 128), step)] if flat else ref.at[index]
+
+    barrier = pltpu.get_barrier_semaphore()
+    greet(barrier, col=partner)
+    for d in range(1, half):
+        greet(barrier, col=2 * ((g + d) % half) + h)
+    if over_rows:
+        for e in range(1, n_rows):
+            greet(barrier, row=(r + e) % n_rows)
+    pl.semaphore_wait(barrier, half + (n_rows - 1 if over_rows else 0))
+
+    order = [*range(1, half), 0]
+    started = []
+    pair = {}
+    for d in order:
+        j = (g + d) % half
+        pair[d] = remote(piece(x_ref, (1 - h) * half + j), pair_buf.at[d], pair_send.at[d], pair_recv.at[d], col=partner)
+        pair[d].start()
+        started.append(pair[d])
+    group = {}
+    for d in order:
+        j = (g + d) % half
+        pair[d].wait_recv()
+        value = piece(x_ref, h * half + j)[...] + pair_buf[d]
+        if d:
+            part[d] = value
+            group[d] = remote(part.at[d], group_buf.at[d], group_send.at[d], group_recv.at[d], col=2 * j + h)
+            group[d].start()
+            started.append(group[d])
+    for d in range(1, half):
+        group[d].wait_recv()
+        value = value + group_buf[d]
+    if over_rows:
+        row_buf[r] = value
+        rows = []
+        for e in range(1, n_rows):
+            rows.append(remote(row_buf.at[r], row_buf.at[r], row_send.at[e], row_recv.at[e], row=(r + e) % n_rows))
+            rows[-1].start()
+        started.extend(rows)
+        for e in range(1, n_rows):
+            source = (r - e + n_rows) % n_rows
+            remote(row_buf.at[source], row_buf.at[source], row_send.at[e], row_recv.at[e], row=source).wait_recv()
+        value = row_buf[0]
+        for e in range(1, n_rows):
+            value = value + row_buf[e]
+    mine = piece(o_ref, h * half + g)
+    mine[...] = value
+    for d in range(1, half):
+        copy = remote(mine, mine, all_send.at[d], all_recv.at[d], col=2 * ((g + d) % half) + h)
+        copy.start()
+        started.append(copy)
+    for d in range(half):
+        j = (g - d + half) % half
+        got = piece(o_ref, h * half + j)
+        if d:
+            remote(got, got, all_send.at[d], all_recv.at[d], col=2 * j + h).wait_recv()
+        copy = remote(got, got, back_send.at[d], back_recv.at[d], col=partner)
+        copy.start()
+        started.append(copy)
+    for d in range(half):
+        got = piece(o_ref, (1 - h) * half + (g - d + half) % half)
+        remote(got, got, back_send.at[d], back_recv.at[d], col=partner).wait_recv()
+    for copy in started:
+        copy.wait_send()
+
+
+def sum_over(value, collective_id, over_rows):
+    n_rows, n_cols = lax.axis_size("row"), lax.axis_size("col")
+    half = n_cols // 2
+    shape = (value.shape[0], value.shape[1] // n_cols) if value.ndim == 2 else value.shape[1:]
+    dma = pltpu.SemaphoreType.DMA
+    return pl.pallas_call(
+        functools.partial(sum_kernel, n_rows, n_cols, over_rows),
+        out_shape=jax.ShapeDtypeStruct(value.shape, jnp.float32),
+        in_specs=[pl.BlockSpec(memory_space=pltpu.VMEM)],
+        out_specs=pl.BlockSpec(memory_space=pltpu.VMEM),
+        scratch_shapes=[pltpu.VMEM((half, *shape), jnp.float32)] * 3
+        + [pltpu.VMEM((n_rows if over_rows else 1, *shape), jnp.float32)]
+        + [dma((half,))] * 4
+        + [dma((n_rows,))] * 2
+        + [dma((half,))] * 4,
+        compiler_params=pltpu.CompilerParams(collective_id=collective_id, has_side_effects=True),
+        name="sum_over",
+    )(value)
+
+
+def total(value, collective_id):
+    n_cols = lax.axis_size("col")
+    rows, cols = value.shape
+    return sum_over(value.reshape(n_cols, rows // n_cols, cols), collective_id, True).reshape(rows, cols)
 
 
 def block_inverse(block):
@@ -123,33 +548,30 @@
 
 
 def local(order, a_matrix, b_matrix, x_block, r_block, p_block):
-    tile_cols = a_matrix.shape[1]
     k = x_block.shape[1]
-    panel = jnp.concatenate([x_block, r_block, p_block], axis=1)
-    matched_t = spread_t(panel.T, tile_cols)
-    prod_a = mm(a_matrix, matched_t, 1, 1, HIGH)
-    prod_b = mm(b_matrix, matched_t, 1, 1, HIGH)
-    grams = total(jnp.concatenate([mm(panel, prod_a, 0, 0), mm(panel, prod_b, 0, 0)], axis=1))
+    panel = jnp.concatenate([x_block.T, r_block.T, p_block.T], axis=0)
+    prod_a, prod_b, tile = apply_both(panel, a_matrix, b_matrix, 0)
+    grams = total(jnp.concatenate([mm(tile, prod_a, 1, 1), mm(tile, prod_b, 1, 1)], axis=1), 1)
     w, ch, kept_a, kept_b = ritz(order, k, grams[:, : 3 * k], grams[:, 3 * k :])
     coords = w[:, :k]
-    resid_t = lax.psum(mm(coords, prod_a, 0, 1) - mm(ch, prod_b, 0, 1), "col")
-    matched_t = spread_t(resid_t, tile_cols)
-    both = mm(panel, w)
-    panel = jnp.concatenate([both[:, :k], resid_t.T, both[:, k:]], axis=1)
-    fresh_a = mm(a_matrix, matched_t, 1, 1, HIGH)
-    fresh_b = mm(b_matrix, matched_t, 1, 1, HIGH)
-    grams = total(jnp.concatenate([mm(panel, fresh_a, 0, 0), mm(panel, fresh_b, 0, 0)], axis=1))
+    resid = gather_sum(mm(coords, prod_a, 0, 0) - mm(ch, prod_b, 0, 0), 2)
+    fresh_a, fresh_b, resid_tile = apply_both(resid, a_matrix, b_matrix, 3)
+    both = mm(w, tile, 0, 0)
+    tile = jnp.concatenate([both[:k], resid_tile, both[k:]], axis=0)
+    grams = total(jnp.concatenate([mm(tile, fresh_a, 1, 1), mm(tile, fresh_b, 1, 1)], axis=1), 4)
     w2, ch2, _, _ = ritz(order, k, extend(kept_a, grams[:, :k]), extend(kept_b, grams[:, k:]))
     c2 = w2[:, :k]
     outer = lambda c: jnp.concatenate([c[:k], c[2 * k :]], axis=0)
     on_a, on_b = mm(w, outer(c2)), mm(w, outer(ch2))
-    resid_t = lax.psum(
-        (mm(on_a, prod_a, 0, 1) + mm(c2[k : 2 * k], fresh_a, 0, 1))
-        - (mm(on_b, prod_b, 0, 1) + mm(ch2[k : 2 * k], fresh_b, 0, 1)),
-        "col",
+    last = gather_sum(
+        (mm(on_a, prod_a, 0, 0) + mm(c2[k : 2 * k], fresh_a, 0, 0))
+        - (mm(on_b, prod_b, 0, 0) + mm(ch2[k : 2 * k], fresh_b, 0, 0)),
+        5,
     )
-    both = mm(panel, w2)
-    return (both[:, :k], resid_t.T, both[:, k:])
+    both = mm(w, panel, 0, 0)
+    panel = jnp.concatenate([both[:k], resid, both[k:]], axis=0)
+    both = mm(w2, panel, 0, 0)
+    return (both[:k].T, last.T, both[k:].T)
 
 
 def solution(mesh):

time: 641 us -> 338 us (0.53); the launches traced: 629 us -> 334 us
  waiting for transfers between devices: 389 us -> 0 us
  Pallas kernels: 59 us -> 286 us
  matrix products: 134 us -> 25.9 us
  between operations: 14.6 us -> 1.25 us
  local copies, waits for them, and re-layouts: 22.6 us -> 12.1 us
    psum x8 -> x0, waiting for transfers between devices: 389 us -> none  [the longest x4 181 us: total(): return lax.psum(lax.psum(value, 'row'), 'col')]
    pallas_call x0 -> x6, Pallas kernels: none -> 227 us  [the longest x2 106 us: gather_sum(): pl.pallas_call(functools.partial(gather_kernel, n_rows, n_cols, chunks),...]
    dot_general x18 -> x15, matrix products: 134 us -> 25.9 us  [mm(): lax.dot_general(left, right, (((lc,), (rc,)), ((), ())), precision=precis...]
  transfers between devices with their start and end apart: 8 -> 0, of which waited for: 8 -> 0; matrix products, arithmetic and copies ran while one was open for 2% -> 0% of each run, Pallas kernels for 0% -> 0%
where the time goes in v1:
time: 338 us; the launch traced here: 334 us
  Pallas kernels  286 us (85%)
  matrix products  25.9 us (8%)
  local copies, waits for them, and re-layouts  12.1 us (4%)
  other arithmetic  8.7 us (3%)
    pallas_call x2, Pallas kernels, gather_sum(): pl.pallas_call(functools.partial(gather_kernel, n_rows, n_cols, chunks),...  106 us
    pallas_call x2, Pallas kernels, apply_both(): pl.pallas_call(functools.partial(apply_kernel, n_rows, n_cols, chunks), o...  79.8 us
    pallas_call x2, Pallas kernels, ritz(): pl.pallas_call(functools.partial(ritz_kernel, order), out_shape=(shape(n,...  59.6 us
    pallas_call x2, Pallas kernels, sum_over(): pl.pallas_call(functools.partial(sum_kernel, n_rows, n_cols, over_rows),...  40.9 us
    dot_general x15, matrix products, mm(): lax.dot_general(left, right, (((lc,), (rc,)), ((), ())), precision=precis...  25.9 us

profile of v1, /device:TPU:13, one launch (start us, length us, event | category | flops | bytes accessed | tf_op | source)
XLA Modules:
  0.0 334.1 jit_solution(72867021137542391)
XLA Ops:
  0.6 3.8 %pad_maximum_fusion.x_ref = f32[192,4096]{1,0:T(8,128)} fusion(f32[64,4096]{1,0:T(8,128)} %bitcast.42, f32[64,4096]{1,0:T(8,128)} %bitcast.44, f32[64,4096]{1,0:T(8,128)} %bitcast.46), kind=kLoop, calls=%fused_computation | loop fusion | flops 1572864 | bytes 6291456 | tf_op jit(solution)/shard_map/concatenate | solution.py:552
  4.4 46.3 %apply_both.2 = (f32[192,2048]{1,0:T(8,128)}, f32[192,2048]{1,0:T(8,128)}, f32[192,2048]{1,0:T(8,128)}) custom-call(f32[192,4096]{1,0:T(8,128)} %pad_maximum_fusion.x_ref, f32[4096,2048]{1,0:T(8,128)} %a_ref.3, f32[4096,2048]{1,0:T(8,128)} %b_ref.3), custom_call_target="tpu_custom_call" | custom-call | tf_op jit(solution)/shard_map/apply_both/pallas_call | solution.py:187
  50.8 3.5 %fusion.36 = f32[192,192]{1,0:T(8,128)S(1)} fusion(f32[192,2048]{1,0:T(8,128)} %get-tuple-element.15, f32[192,2048]{1,0:T(8,128)} %get-tuple-element.17), kind=kOutput, calls=%fused_computation.53 | convolution fusion | flops 905969664 | bytes 3293184 | tf_op jit(solution)/shard_map/dot_general | solution.py:17
  54.3 1.4 fusion.35
  55.7 0.8 pad_maximum_fusion.4
  56.5 24.3 %sum_over.2 = f32[8,24,384]{2,1,0:T(8,128)} custom-call(f32[8,24,384]{2,1,0:T(8,128)} %bitcast.49), custom_call_target="tpu_custom_call" | custom-call | tf_op jit(solution)/shard_map/sum_over/pallas_call | solution.py:438
  80.8 1.8 fusion.29
  82.7 29.9 %ritz.2 = (f32[192,128]{1,0:T(8,128)}, f32[192,64]{1,0:T(8,128)}, f32[128,128]{1,0:T(8,128)}, f32[128,128]{1,0:T(8,128)}) custom-call(f32[192,192]{1,0:T(8,128)} %get-tuple-element.34.ga_ref, f32[192,192]{1,0:T(8,128)} %get-tuple-element.33.gb_ref), custom_call_target="tpu_custom_call" | custom-call | tf_op jit(solution)/shard_map/ritz/pallas_call | solution.py:527
  112.6 2.0 fusion.37
  114.6 1.1 fusion.28
  115.7 0.8 fusion.33
  116.5 1.1 fusion.9
  117.6 1.9 convolution_subtract_fusion.x_ref
  119.5 53.1 %gather_sum.2.x_ref = f32[64,4096]{1,0:T(8,128)} custom-call(f32[64,2048]{1,0:T(8,128)} %convolution_subtract_fusion.x_ref), custom_call_target="tpu_custom_call" | custom-call | tf_op jit(solution)/shard_map/gather_sum/pallas_call | solution.py:344
  172.6 33.5 %apply_both.3 = (f32[64,2048]{1,0:T(8,128)}, f32[64,2048]{1,0:T(8,128)}, f32[64,2048]{1,0:T(8,128)}) custom-call(f32[64,4096]{1,0:T(8,128)} %gather_sum.2.x_ref, f32[4096,2048]{1,0:T(8,128)} %a_ref.3, f32[4096,2048]{1,0:T(8,128)} %b_ref.3), custom_call_target="tpu_custom_call" | custom-call | tf_op jit(solution)/shard_map/apply_both/pallas_call | solution.py:187
  206.2 0.0 copy-start.4
  206.2 0.0 copy-start.5
  206.2 3.3 fusion.7
  209.5 0.0 copy-done.4
  209.5 0.0 copy-done.5
  209.5 0.0 copy-done.9
  209.5 1.6 fusion.8
  211.2 0.7 copy.22
  211.9 16.6 %sum_over.3 = f32[8,24,128]{2,1,0:T(8,128)} custom-call(f32[8,24,128]{2,1,0:T(8,128)} %bitcast.51), custom_call_target="tpu_custom_call" | custom-call | tf_op jit(solution)/shard_map/sum_over/pallas_call | solution.py:438
  228.6 1.6 fusion.32
  230.1 0.7 copy.27
  230.8 0.7 copy.28
  231.5 0.8 pad_maximum_fusion.6
  232.3 0.1 copy.24
  232.4 1.6 maximum_maximum_fusion.ga_ref
  234.1 0.1 copy.26
  234.1 1.6 maximum_maximum_fusion.1.gb_ref
  235.7 29.6 %ritz.3 = (f32[192,128]{1,0:T(8,128)}, f32[192,64]{1,0:T(8,128)}, f32[128,128]{1,0:T(8,128)}, f32[128,128]{1,0:T(8,128)}) custom-call(f32[192,192]{1,0:T(8,128)} %maximum_maximum_fusion.ga_ref, f32[192,192]{1,0:T(8,128)} %maximum_maximum_fusion.1.gb_ref), custom_call_target="tpu_custom_call" | custom-call | tf_op jit(solution)/shard_map/ritz/pallas_call | solution.py:527
  265.4 0.8 fusion.30
  266.2 0.2 fusion.15
  266.4 1.1 fusion.39
  267.6 0.2 fusion.11
  267.8 1.1 fusion.38
  269.0 0.6 convolution_add_fusion.1
  269.6 0.0 copy-start.7
  269.6 2.3 fusion.6.x_ref
  271.9 52.7 %gather_sum.3 = f32[64,4096]{1,0:T(8,128)} custom-call(f32[64,2048]{1,0:T(8,128)} %fusion.6.x_ref), custom_call_target="tpu_custom_call" | custom-call | tf_op jit(solution)/shard_map/gather_sum/pallas_call | solution.py:344
  324.6 3.5 %fusion.26 = f32[128,4096]{1,0:T(8,128)S(1)} fusion(f32[192,128]{1,0:T(8,128)S(1)} %copy-done.8, f32[64,4096]{1,0:T(8,128)S(1)} %bitcast.43, f32[64,4096]{1,0:T(8,128)} %bitcast.45, f32[64,4096]{1,0:T(8,128)} %bitcast.47), kind=kOutput, calls=%fused_computation.43 | convolution fusion | flops 1209532416 | bytes 5341184 | tf_op jit(solution)/shard_map/dot_general | solution.py:17
  328.2 0.1 fusion.27
  328.3 1.1 copy-done.3
  329.4 2.0 fusion
  331.4 1.5 slice_bitcast_fusion
  332.9 1.0 copy.30
  (29 shorter events, 0.1 us)
Async XLA Ops:
  50.7 3.5 %copy-start = (f32[192,2048]{1,0:T(8,128)S(1)}, f32[192,2048]{1,0:T(8,128)}, u32[]{:S(2)}) copy-start(f32[192,2048]{1,0:T(8,128)} %get-tuple-element.16) | copy-start | bytes 4718596
  50.8 3.5 %copy-start.2 = (f32[192,2048]{1,0:T(8,128)S(1)}, f32[192,2048]{1,0:T(8,128)}, u32[]{:S(2)}) copy-start(f32[192,2048]{1,0:T(8,128)} %get-tuple-element.15) | copy-start | bytes 4718596
  114.6 1.1 copy-start.14
  114.6 1.1 copy-start.15
  114.6 1.9 copy-start.8
  115.7 1.9 copy-start.1
  115.7 1.9 copy-start.16
  206.2 3.3 copy-start.4
  206.2 3.3 copy-start.5
  206.2 3.3 copy-start.9
  206.2 3.3 copy-start.12
  265.4 2.2 copy-start.13
  267.6 1.4 copy-start.10
  267.8 1.8 copy-start.11
  269.6 55.0 %copy-start.7 = (f32[4096,64]{0,1:T(8,128)S(1)}, f32[4096,64]{0,1:T(8,128)}, u32[]{:S(2)}) copy-start(f32[4096,64]{0,1:T(8,128)} %param.9) | copy-start | bytes 3145732
  328.2 1.2 copy-start.3
  331.4 1.5 copy-start.6

commit v2 on v1

--- a/solution.py
+++ b/solution.py
@@ -64,12 +64,12 @@
 
 
 def apply_kernel(
-    n_rows, n_cols, chunks, x_ref, a_ref, b_ref, on_a_ref, on_b_ref, tile_ref, x_parts, tile, up_sems, down_sems, recv_sems
+    n_rows, n_cols, chunks, steps, x_ref, a_ref, b_ref, out_ref, tile_ref, x_parts, tile, up_sems, down_sems, recv_sems
 ):
     n, k = pl.program_id(0), pl.program_id(1)
     depth = pl.num_programs(1)
     now = n * depth + k
-    steps = chunks
+    per = chunks // steps
     m, tk = x_ref.shape[0], a_ref.shape[0]
     r, c = lax.axis_index("row"), lax.axis_index("col")
     ratio = n_cols // n_rows
@@ -125,7 +125,7 @@
         x_parts[:m] = high
         x_parts[m:] = low
 
-    for mat_ref, out_ref in ((a_ref, on_a_ref), (b_ref, on_b_ref)):
+    for at, mat_ref in enumerate((a_ref, b_ref)):
         high, low = halves(mat_ref[...])
         x = x_parts[:, pl.ds(pl.multiple_of(k * tk, 128), tk)]
         both = dot(x, high)
@@ -133,18 +133,19 @@
 
         @pl.when(k == 0)
         def _():
-            out_ref[...] = value
+            out_ref[at * m : (at + 1) * m] = value
 
         @pl.when(k > 0)
         def _():
-            out_ref[...] += value
+            out_ref[at * m : (at + 1) * m] += value
 
     for away in range(1, n_rows):
-        lag = 2 * away
-
-        @pl.when(((r == home + away) | (r == home - away)) & (now >= lag) & (now < chunks + lag))
-        def _():
-            relay(now - lag)
+        for i in range(per):
+            chunk = per * now + i - 2 * away
+
+            @pl.when(((r == home + away) | (r == home - away)) & (chunk >= 0) & (chunk < chunks))
+            def _():
+                relay(chunk)
 
     @pl.when(now == steps - 1)
     def _():
@@ -152,7 +153,7 @@
 
             @pl.when((r == home + away) | (r == home - away))
             def _():
-                for i in range(max(steps - 2 * away, 0), chunks):
+                for i in range(max(chunks - 2 * away, 0), chunks):
                     relay(i)
 
         @pl.when((r >= home) & has_up)
@@ -172,24 +173,27 @@
         @pl.when(r != home)
         def _():
             tile_ref[...] = tile[...]
+
+
+TK, TN = 4096, 256
 
 
 def apply_both(x_rows, a_matrix, b_matrix, collective_id):
     n_rows, n_cols = lax.axis_size("row"), lax.axis_size("col")
     m, rows = x_rows.shape
     cols = a_matrix.shape[1]
-    tk, tn = min(1024, rows), min(512, cols)
+    tk, tn = min(TK, rows), min(TN, cols)
     grid = (cols // tn, rows // tk)
-    chunks = grid[0] * grid[1]
+    steps = grid[0] * grid[1]
+    chunks = max(steps, cols // 128)
     block = pl.BlockSpec((tk, tn), lambda n, k: (k, n))
-    out = pl.BlockSpec((m, tn), lambda n, k: (0, n))
-    shape = jax.ShapeDtypeStruct((m, cols), jnp.float32)
+    shape = lambda rows: jax.ShapeDtypeStruct((rows, cols), jnp.float32)
     return pl.pallas_call(
-        functools.partial(apply_kernel, n_rows, n_cols, chunks),
-        out_shape=(shape,) * 3,
+        functools.partial(apply_kernel, n_rows, n_cols, chunks, steps),
+        out_shape=(shape(2 * m), shape(m)),
         grid=grid,
         in_specs=[pl.BlockSpec(memory_space=pltpu.VMEM), block, block],
-        out_specs=[out, out, pl.BlockSpec(memory_space=pltpu.VMEM)],
+        out_specs=[pl.BlockSpec((2 * m, tn), lambda n, k: (0, n)), pl.BlockSpec(memory_space=pltpu.VMEM)],
         scratch_shapes=[pltpu.VMEM((2 * m, rows), jnp.bfloat16), pltpu.VMEM((m, cols), jnp.float32)]
         + [pltpu.SemaphoreType.DMA((chunks,))] * 3,
         compiler_params=pltpu.CompilerParams(
@@ -197,9 +201,6 @@
         ),
         name="apply_both",
     )(x_rows, a_matrix, b_matrix)
-
-
-LAG = 3
 
 
 def gather_kernel(n_rows, n_cols, chunks, x_ref, o_ref, from_up, from_down, inward, row_send, up_recv, down_recv, send, recv):
@@ -310,14 +311,13 @@
                     def _():
                         copy.start()
 
-    for i in range(chunks + LAG):
-        if i < chunks:
-            reduce(i)
-            for p in range(ratio):
-                broadcast(p, i, True)
-        if i >= LAG:
-            for p in range(ratio):
-                broadcast(p, i - LAG, False)
+    for i in range(chunks):
+        reduce(i)
+        for p in range(ratio):
+            broadcast(p, i, True)
+    for i in range(chunks):
+        for p in range(ratio):
+            broadcast(p, i, False)
     for k in range(chunks):
         @pl.when(r > home)
         def _():
@@ -453,29 +453,41 @@
 def total(value, collective_id):
     n_cols = lax.axis_size("col")
     rows, cols = value.shape
-    return sum_over(value.reshape(n_cols, rows // n_cols, cols), collective_id, True).reshape(rows, cols)
+    return sum_over(value.reshape(n_cols, rows // n_cols, cols), collective_id, True)
+
+
+PANEL = 8
 
 
 def block_inverse(block):
     size = block.shape[0]
-    rows = lax.broadcasted_iota(jnp.int32, (size, size), 0)
-    cols = lax.broadcasted_iota(jnp.int32, (size, size), 1)
-    inverse = jnp.where(rows == cols, 1.0, 0.0)
-    for j in range(size):
-        pivot = 1.0 / block[j : j + 1, j : j + 1]
-        factor = jnp.where(rows[:, :1] > j, block[:, j : j + 1], 0.0)
-        inverse = inverse - factor * (inverse[j : j + 1] * pivot)
-        block = block - factor * (block[j : j + 1] * pivot)
-    diag = jnp.sum(jnp.where(rows == cols, block, 0.0), axis=1, keepdims=True)
-    return inverse / jnp.sqrt(diag)
-
-
-def ritz_kernel(order, ga_ref, gb_ref, w_ref, ch_ref, wa_ref, wb_ref, linv_ref, sym_ref):
-    n, k = w_ref.shape[0], ch_ref.shape[1]
-    gb = gb_ref[...]
-    sym_ref[...] = 0.5 * (gb + gb.T)
-    ga = ga_ref[...]
-    ga = 0.5 * (ga + ga.T)
+    shape = (size, 2 * size)
+    rows = lax.broadcasted_iota(jnp.int32, shape, 0)
+    cols = lax.broadcasted_iota(jnp.int32, shape, 1)
+    ident = jnp.where(rows == cols, 1.0, 0.0)[:, :size]
+    work = jnp.concatenate([block, ident], axis=1)
+    for start in range(0, size, PANEL):
+        spread = [jnp.broadcast_to(work[:, start + i : start + i + 1], shape) for i in range(PANEL)]
+        for i in range(PANEL):
+            j = start + i
+            column = spread[i]
+            factor = jnp.where(rows > j, column, 0.0) * (1.0 / column[j : j + 1])
+            for later in range(i + 1, PANEL):
+                spread[later] = spread[later] - factor * column[start + later : start + later + 1]
+            work = work - factor * work[j : j + 1]
+    diag = jnp.sum(jnp.where(rows == cols, work, 0.0), axis=1, keepdims=True)
+    return work[:, size:] / jnp.sqrt(diag)
+
+
+def mm_split(left, right):
+    left_high, left_low = halves(left)
+    right_high, right_low = halves(right)
+    return dot(left_high, right_high) + (dot(left_high, right_low) + dot(left_low, right_high))
+
+
+def solve(order, k, ga, gb, linv_ref, sym_ref):
+    n = ga.shape[0]
+    sym_ref[...] = gb
     nb = n // k
     cut = lambda ref, i, j: ref[i * k : (i + 1) * k, j * k : (j + 1) * k]
     linv_ref[...] = jnp.zeros((n, n), jnp.float32)
@@ -508,69 +520,102 @@
     centred = middle - shift * ident
     sign_est = centred / jnp.sqrt(jnp.full((1, 1), jnp.sum(centred * centred) + 1e-06))
     for turn in range(NS_STEPS):
-        sign_est = 1.5 * sign_est - 0.5 * mm(sign_est, mm(sign_est, sign_est))
+        sign_est = 1.5 * sign_est - 0.5 * mm_split(sign_est, mm_split(sign_est, sign_est))
     filtered = (0.5 * (ident - sign_est))[:, :k]
     coords = mm(linv_t, filtered) * math.sqrt(order)
     reduced = mm(filtered.T, mm(middle, filtered))
-    ch_ref[...] = mm(coords, reduced)
+    return coords, mm(coords, reduced)
+
+
+def outer_rows(value, k):
+    return jnp.where((lax.broadcasted_iota(jnp.int32, value.shape, 0) >= k), value, 0.0)
+
+
+def first_kernel(order, grams_ref, w_ref, mix_ref, wa_ref, wb_ref, linv_ref, sym_ref):
+    n, k = w_ref.shape[0], mix_ref.shape[1]
+    grams = grams_ref[...].reshape(2 * n, n)
+    ga, gb = grams[:n], grams[n:]
+    ga, gb = 0.5 * (ga + ga.T), 0.5 * (gb + gb.T)
+    coords, reduced = solve(order, k, ga, gb, linv_ref, sym_ref)
+    mix_ref[:n] = coords
+    mix_ref[n:] = -reduced
     w_ref[:, :k] = coords
-    w_ref[:, k:] = jnp.where(lax.broadcasted_iota(jnp.int32, (n, k), 0) >= k, coords, 0.0)
+    w_ref[:, k:] = outer_rows(coords, k)
     w = w_ref[...]
     w_t = w.T
     wa_ref[...] = mm(w_t, mm(ga, w))
     wb_ref[...] = mm(w_t, mm(sym_ref[...], w))
 
 
-def ritz(order, width, gram_a, gram_b):
-    n, k = gram_a.shape[0], width
-    shape = lambda *dims: jax.ShapeDtypeStruct(dims, jnp.float32)
+def second_kernel(order, wa_ref, wb_ref, w_ref, grams_ref, wide_ref, inner_ref, mix_ref, mix_in_ref, linv_ref, sym_ref, ga_ref, c_ref):
+    n, k = w_ref.shape[0], mix_ref.shape[1]
+    grams = grams_ref[...].reshape(2 * k, n + k)
+    w = w_ref[...]
+    for at, kept in enumerate((wa_ref, wb_ref)):
+        fresh = grams[at * k : (at + 1) * k]
+        ends = mm(fresh[:, :n], w)
+        middle = fresh[:, n:]
+        full = ga_ref.at[at]
+        full[:k, :k] = kept[:k, :k]
+        full[:k, 2 * k :] = kept[:k, k:]
+        full[2 * k :, :k] = kept[k:, :k]
+        full[2 * k :, 2 * k :] = kept[k:, k:]
+        full[k : 2 * k, :k] = ends[:, :k]
+        full[k : 2 * k, 2 * k :] = ends[:, k:]
+        full[k : 2 * k, k : 2 * k] = middle
+        full[:k, k : 2 * k] = ends[:, :k].T
+        full[2 * k :, k : 2 * k] = ends[:, k:].T
+    ga, gb = ga_ref[0], ga_ref[1]
+    ga, gb = 0.5 * (ga + ga.T), 0.5 * (gb + gb.T)
+    coords, reduced = solve(order, k, ga, gb, linv_ref, sym_ref)
+    c_ref[:, :k] = coords
+    c_ref[:, k : 2 * k] = outer_rows(coords, k)
+    c_ref[:, 2 * k :] = reduced
+    ends = mm(w[:, :k], c_ref[:k]) + mm(w[:, k:], c_ref[2 * k :])
+    wide_ref[...] = ends[:, : 2 * k]
+    inner_ref[...] = c_ref[k : 2 * k, : 2 * k]
+    mix_ref[:n] = ends[:, :k]
+    mix_ref[n:] = -ends[:, 2 * k :]
+    mix_in_ref[:k] = c_ref[k : 2 * k, :k]
+    mix_in_ref[k:] = -c_ref[k : 2 * k, 2 * k :]
+
+
+def in_vmem(kernel, shapes, scratch, name, *args):
     return pl.pallas_call(
-        functools.partial(ritz_kernel, order),
-        out_shape=(shape(n, 2 * k), shape(n, k), shape(2 * k, 2 * k), shape(2 * k, 2 * k)),
-        in_specs=[pl.BlockSpec(memory_space=pltpu.VMEM)] * 2,
-        out_specs=[pl.BlockSpec(memory_space=pltpu.VMEM)] * 4,
-        scratch_shapes=[pltpu.VMEM((n, n), jnp.float32)] * 2,
-        name="ritz",
-    )(gram_a, gram_b)
-
-
-def extend(kept, fresh):
-    k = fresh.shape[1]
-    x, r, p = fresh[:k], fresh[k : 2 * k], fresh[2 * k :]
-    return jnp.concatenate(
-        [
-            jnp.concatenate([kept[:k, :k], x, kept[:k, k:]], axis=1),
-            jnp.concatenate([x.T, r, p.T], axis=1),
-            jnp.concatenate([kept[k:, :k], p, kept[k:, k:]], axis=1),
-        ],
-        axis=0,
-    )
+        kernel,
+        out_shape=tuple(jax.ShapeDtypeStruct(dims, jnp.float32) for dims in shapes),
+        in_specs=[pl.BlockSpec(memory_space=pltpu.VMEM)] * len(args),
+        out_specs=[pl.BlockSpec(memory_space=pltpu.VMEM)] * len(shapes),
+        scratch_shapes=[pltpu.VMEM(dims, jnp.float32) for dims in scratch],
+        name=name,
+    )(*args)
+
+
+def first_ritz(order, k, grams):
+    n = grams.shape[-1]
+    shapes = ((n, 2 * k), (2 * n, k), (2 * k, 2 * k), (2 * k, 2 * k))
+    return in_vmem(functools.partial(first_kernel, order), shapes, [(n, n)] * 2, "first_ritz", grams)
+
+
+def second_ritz(order, k, kept_a, kept_b, w, grams):
+    n = w.shape[0]
+    shapes = ((n, 2 * k), (k, 2 * k), (2 * n, k), (2 * k, k))
+    scratch = [(n, n)] * 2 + [(2, n, n), (n, 3 * k)]
+    return in_vmem(functools.partial(second_kernel, order), shapes, scratch, "second_ritz", kept_a, kept_b, w, grams)
 
 
 def local(order, a_matrix, b_matrix, x_block, r_block, p_block):
     k = x_block.shape[1]
     panel = jnp.concatenate([x_block.T, r_block.T, p_block.T], axis=0)
-    prod_a, prod_b, tile = apply_both(panel, a_matrix, b_matrix, 0)
-    grams = total(jnp.concatenate([mm(tile, prod_a, 1, 1), mm(tile, prod_b, 1, 1)], axis=1), 1)
-    w, ch, kept_a, kept_b = ritz(order, k, grams[:, : 3 * k], grams[:, 3 * k :])
-    coords = w[:, :k]
-    resid = gather_sum(mm(coords, prod_a, 0, 0) - mm(ch, prod_b, 0, 0), 2)
-    fresh_a, fresh_b, resid_tile = apply_both(resid, a_matrix, b_matrix, 3)
-    both = mm(w, tile, 0, 0)
-    tile = jnp.concatenate([both[:k], resid_tile, both[k:]], axis=0)
-    grams = total(jnp.concatenate([mm(tile, fresh_a, 1, 1), mm(tile, fresh_b, 1, 1)], axis=1), 4)
-    w2, ch2, _, _ = ritz(order, k, extend(kept_a, grams[:, :k]), extend(kept_b, grams[:, k:]))
-    c2 = w2[:, :k]
-    outer = lambda c: jnp.concatenate([c[:k], c[2 * k :]], axis=0)
-    on_a, on_b = mm(w, outer(c2)), mm(w, outer(ch2))
-    last = gather_sum(
-        (mm(on_a, prod_a, 0, 0) + mm(c2[k : 2 * k], fresh_a, 0, 0))
-        - (mm(on_b, prod_b, 0, 0) + mm(ch2[k : 2 * k], fresh_b, 0, 0)),
-        5,
-    )
-    both = mm(w, panel, 0, 0)
-    panel = jnp.concatenate([both[:k], resid, both[k:]], axis=0)
-    both = mm(w2, panel, 0, 0)
+    prods, tile = apply_both(panel, a_matrix, b_matrix, 0)
+    grams = total(mm(prods, tile, 1, 1, HIGH), 1)
+    w, mix, kept_a, kept_b = first_ritz(order, k, grams)
+    resid = gather_sum(mm(mix, prods, 0, 0, HIGH), 2)
+    fresh, resid_tile = apply_both(resid, a_matrix, b_matrix, 3)
+    grams = total(mm(fresh, jnp.concatenate([tile, resid_tile], axis=0), 1, 1, HIGH), 4)
+    wide, inner, mix, mix_in = second_ritz(order, k, kept_a, kept_b, w, grams)
+    last = gather_sum(mm(mix, prods, 0, 0, HIGH) + mm(mix_in, fresh, 0, 0, HIGH), 5)
+    both = mm(wide, panel, 0, 0, HIGH) + mm(inner, resid, 0, 0, HIGH)
     return (both[:k].T, last.T, both[k:].T)
 
 

time: 338 us -> 258 us (0.76); the launches traced: 334 us -> 258 us
  Pallas kernels: 286 us -> 232 us
  local copies, waits for them, and re-layouts: 12.1 us -> 2.58 us
  matrix products: 25.9 us -> 18 us
  other arithmetic: 8.7 us -> 3.83 us
    pallas_call x4, Pallas kernels: 139 us -> 107 us  [the longest x2 74.3 us: apply_both(): pl.pallas_call(functools.partial(apply_kernel, n_rows, n_cols, chunks, st...]
    pallas_call x2, Pallas kernels: 106 us -> 80.9 us  [gather_sum(): pl.pallas_call(functools.partial(gather_kernel, n_rows, n_cols, chunks),...]
    dot_general x15 -> x7, matrix products: 25.9 us -> 18 us  [mm(): lax.dot_general(left, right, (((lc,), (rc,)), ((), ())), precision=precis...]
    slice x7 -> x0, local copies, waits for them, and re-layouts: 6.2 us -> none  [the longest x1 1.82 us: local(): w, ch, kept_a, kept_b = ritz(order, k, grams[:, :3 * k], grams[:, 3 * k:])]
    concatenate x5 -> x0, other arithmetic: 4.9 us -> none  [the longest x2 3.23 us: extend(): jnp.concatenate([jnp.concatenate([kept[:k, :k], x, kept[:k, k:]], axis=1)...]
where the time goes in v2:
time: 258 us
  Pallas kernels  232 us (90%)
  matrix products  18 us (7%)
  other arithmetic  3.83 us (1%)
  local copies, waits for them, and re-layouts  2.58 us (1%)
    pallas_call x2, Pallas kernels, gather_sum(): pl.pallas_call(functools.partial(gather_kernel, n_rows, n_cols, chunks),...  80.9 us
    pallas_call x2, Pallas kernels, apply_both(): pl.pallas_call(functools.partial(apply_kernel, n_rows, n_cols, chunks, st...  74.3 us
    pallas_call x2, Pallas kernels, sum_over(): pl.pallas_call(functools.partial(sum_kernel, n_rows, n_cols, over_rows),...  44.2 us
    pallas_call x2, Pallas kernels, in_vmem(): pl.pallas_call(kernel, out_shape=tuple((jax.ShapeDtypeStruct(dims, jnp.fl...  33 us
    dot_general x7, matrix products, mm(): lax.dot_general(left, right, (((lc,), (rc,)), ((), ())), precision=precis...  18 us

profile of v2, /device:TPU:13, one launch (start us, length us, event | category | flops | bytes accessed | tf_op | source)
XLA Modules:
  0.0 257.6 jit_solution(4100652743081732416)
XLA Ops:
  0.6 3.8 %pad_maximum_fusion.x_ref = f32[192,4096]{1,0:T(8,128)} fusion(f32[64,4096]{1,0:T(8,128)} %bitcast.23, f32[64,4096]{1,0:T(8,128)} %bitcast.25, f32[64,4096]{1,0:T(8,128)} %bitcast.27), kind=kLoop, calls=%fused_computation.1 | loop fusion | flops 1572864 | bytes 6291456 | tf_op jit(solution)/shard_map/concatenate | solution.py:609
  4.5 46.5 %apply_both.2 = (f32[384,2048]{1,0:T(8,128)}, f32[192,2048]{1,0:T(8,128)}) custom-call(f32[192,4096]{1,0:T(8,128)} %pad_maximum_fusion.x_ref, f32[4096,2048]{1,0:T(8,128)} %a_ref.3, f32[4096,2048]{1,0:T(8,128)} %b_ref.3), custom_call_target="tpu_custom_call" | custom-call | tf_op jit(solution)/shard_map/apply_both/pallas_call | solution.py:191
  51.0 0.0 copy-start
  51.0 4.7 %fusion.6 = f32[384,192]{1,0:T(8,128)} fusion(f32[384,2048]{1,0:T(8,128)} %get-tuple-element.15, f32[192,2048]{1,0:T(8,128)} %get-tuple-element.16), kind=kOutput, calls=%fused_computation.11 | convolution fusion | flops 905969664 | bytes 5013504 | tf_op jit(solution)/shard_map/dot_general | solution.py:17
  55.7 26.7 %sum_over.2.grams_ref = f32[8,48,192]{2,1,0:T(8,128)} custom-call(f32[8,48,192]{2,1,0:T(8,128)} %bitcast.29), custom_call_target="tpu_custom_call" | custom-call | tf_op jit(solution)/shard_map/sum_over/pallas_call | solution.py:438
  82.4 16.4 %first_ritz.1 = (f32[192,128]{1,0:T(8,128)}, f32[384,64]{1,0:T(8,128)}, f32[128,128]{1,0:T(8,128)}, f32[128,128]{1,0:T(8,128)}) custom-call(f32[8,48,192]{2,1,0:T(8,128)} %sum_over.2.grams_ref), custom_call_target="tpu_custom_call" | custom-call | tf_op jit(solution)/shard_map/first_ritz/pallas_call | solution.py:584
  98.8 0.0 copy-done
  98.8 2.8 %fusion.7.x_ref = f32[64,2048]{1,0:T(8,128)} fusion(f32[384,64]{1,0:T(8,128)} %get-tuple-element.20, f32[384,2048]{1,0:T(8,128)S(1)} %copy-done), kind=kOutput, calls=%fused_computation.12 | convolution fusion | flops 301989888 | bytes 3768320 | tf_op jit(solution)/shard_map/dot_general | solution.py:17
  101.6 40.5 %gather_sum.2.x_ref = f32[64,4096]{1,0:T(8,128)} custom-call(f32[64,2048]{1,0:T(8,128)} %fusion.7.x_ref), custom_call_target="tpu_custom_call" | custom-call | tf_op jit(solution)/shard_map/gather_sum/pallas_call | solution.py:344
  142.1 27.8 %apply_both.3 = (f32[128,2048]{1,0:T(8,128)}, f32[64,2048]{1,0:T(8,128)}) custom-call(f32[64,4096]{1,0:T(8,128)} %gather_sum.2.x_ref, f32[4096,2048]{1,0:T(8,128)} %a_ref.3, f32[4096,2048]{1,0:T(8,128)} %b_ref.3), custom_call_target="tpu_custom_call" | custom-call | tf_op jit(solution)/shard_map/apply_both/pallas_call | solution.py:191
  169.9 3.7 %fusion = f32[128,256]{1,0:T(8,128)} fusion(f32[128,2048]{1,0:T(8,128)} %get-tuple-element.21, f32[64,2048]{1,0:T(8,128)} %get-tuple-element.22, f32[192,2048]{1,0:T(8,128)} %get-tuple-element.16), kind=kOutput, calls=%fused_computation.3 | convolution fusion | flops 403177472 | bytes 3276800 | tf_op jit(solution)/shard_map/dot_general | solution.py:17
  173.6 17.5 %sum_over.3.grams_ref = f32[8,16,256]{2,1,0:T(8,128)} custom-call(f32[8,16,256]{2,1,0:T(8,128)} %bitcast.30), custom_call_target="tpu_custom_call" | custom-call | tf_op jit(solution)/shard_map/sum_over/pallas_call | solution.py:438
  191.1 16.7 %second_ritz.1 = (f32[192,128]{1,0:T(8,128)}, f32[64,128]{1,0:T(8,128)}, f32[384,64]{1,0:T(8,128)}, f32[128,64]{1,0:T(8,128)}) custom-call(f32[128,128]{1,0:T(8,128)} %get-tuple-element.17.wa_ref, f32[128,128]{1,0:T(8,128)} %get-tuple-element.18.wb_ref, f32[192,128]{1,0:T(8,128)} %get-tuple-element.19.w_ref, f32[8,16,256]{2,1,0:T(8,128)} %sum_over.3.grams_ref), custom_call_target="tpu_custom_call" | custom-call | tf_op jit(solution)/shard_map/second_ritz/pallas_call | solution.py:584
  207.8 0.0 copy-start.2
  207.8 0.0 copy-start.7
  207.8 0.0 copy-start.6
  207.8 2.1 fusion.8
  209.9 0.0 copy-done.2
  209.9 0.0 copy-done.7
  209.9 0.0 copy-start.4
  209.9 0.0 copy-start.5
  209.9 1.3 convolution_add_fusion.1.x_ref
  211.2 0.0 copy-start.1
  211.2 0.0 copy-start.8
  211.2 40.4 %gather_sum.3 = f32[64,4096]{1,0:T(8,128)} custom-call(f32[64,2048]{1,0:T(8,128)} %convolution_add_fusion.1.x_ref), custom_call_target="tpu_custom_call" | custom-call | tf_op jit(solution)/shard_map/gather_sum/pallas_call | solution.py:344
  251.6 0.0 copy-done.6
  251.6 0.0 copy-done.4
  251.6 0.0 copy-done.5
  251.6 2.3 fusion.5
  254.0 0.0 copy-done.1
  254.0 0.0 copy-done.8
  254.0 1.1 convolution_add_fusion
  255.1 0.0 copy-start.3
  255.1 1.5 slice_bitcast_fusion
  256.6 0.1 copy-done.3
  256.7 1.0 copy.11
Async XLA Ops:
  51.0 47.8 %copy-start = (f32[384,2048]{1,0:T(8,128)S(1)}, f32[384,2048]{1,0:T(8,128)}, u32[]{:S(2)}) copy-start(f32[384,2048]{1,0:T(8,128)} %get-tuple-element.15) | copy-start | bytes 9437188
  207.8 2.1 copy-start.2
  207.8 2.1 copy-start.7
  207.8 43.8 %copy-start.6 = (f32[192,128]{1,0:T(8,128)S(1)}, f32[192,128]{1,0:T(8,128)}, u32[]{:S(2)}) copy-start(f32[192,128]{1,0:T(8,128)} %get-tuple-element.23) | copy-start | bytes 294916
  209.9 41.7 %copy-start.4 = (f32[4096,64]{0,1:T(8,128)S(1)}, f32[4096,64]{0,1:T(8,128)}, u32[]{:S(2)}) copy-start(f32[4096,64]{0,1:T(8,128)} %param.9) | copy-start | bytes 3145732
  209.9 41.7 %copy-start.5 = (f32[4096,64]{0,1:T(8,128)S(1)}, f32[4096,64]{0,1:T(8,128)}, u32[]{:S(2)}) copy-start(f32[4096,64]{0,1:T(8,128)} %param.8) | copy-start | bytes 3145732
  211.2 42.7 %copy-start.1 = (f32[64,4096]{1,0:T(8,128)S(1)}, f32[64,4096]{1,0:T(8,128)}, u32[]{:S(2)}) copy-start(f32[64,4096]{1,0:T(8,128)} %gather_sum.2.x_ref) | copy-start | bytes 3145732
  211.2 42.7 %copy-start.8 = (f32[64,128]{1,0:T(8,128)S(1)}, f32[64,128]{1,0:T(8,128)}, u32[]{:S(2)}) copy-start(f32[64,128]{1,0:T(8,128)} %get-tuple-element.24) | copy-start | bytes 98308
  255.1 1.6 copy-start.3

commit v3 on v2

--- a/solution.py
+++ b/solution.py
@@ -1,4 +1,5 @@
 import functools
+import itertools
 import math
 
 import jax
@@ -63,63 +64,58 @@
     return lax.dot_general(left, right, (((lc,), (rc,)), ((), ())), preferred_element_type=jnp.float32)
 
 
-def apply_kernel(
-    n_rows, n_cols, chunks, steps, x_ref, a_ref, b_ref, out_ref, tile_ref, x_parts, tile, up_sems, down_sems, recv_sems
-):
+def mirror_pairs(n):
+    pairs = list(itertools.combinations(range(n), 2))
+    if len(pairs) > 6:
+        return [(low, high) for low, high in pairs]
+    best = None
+    for flips in itertools.product((False, True), repeat=len(pairs)):
+        chosen = [(high, low) if flip else (low, high) for flip, (low, high) in zip(flips, pairs)]
+        loads = {}
+        for row, home in chosen:
+            for z in range(min(row, home), max(row, home)):
+                link = (home, row > home, z)
+                loads[link] = loads.get(link, 0) + 1
+        if best is None or max(loads.values()) < best[0]:
+            best = (max(loads.values()), chosen)
+    return best[1]
+
+
+def apply_kernel(n_rows, n_cols, steps, x_ref, a_ref, b_ref, out_ref, tile_ref, x_parts, tile, send_sems, recv_sem):
     n, k = pl.program_id(0), pl.program_id(1)
-    depth = pl.num_programs(1)
-    now = n * depth + k
-    per = chunks // steps
+    now = n * pl.num_programs(1) + k
     m, tk = x_ref.shape[0], a_ref.shape[0]
     r, c = lax.axis_index("row"), lax.axis_index("col")
     ratio = n_cols // n_rows
     home, part = c // ratio, c % ratio
     width = tile.shape[1]
-    step = width // chunks
-    has_up, has_down = r < n_rows - 1, r > 0
-
-    def slot(i):
-        return tile.at[:, pl.ds(pl.multiple_of(i * step, 128), step)]
-
-    def up(i, src):
-        return remote(src, slot(i), up_sems.at[i], recv_sems.at[i], row=r + 1)
-
-    def down(i, src):
-        return remote(src, slot(i), down_sems.at[i], recv_sems.at[i], row=r - 1)
-
-    def relay(i):
-        @pl.when(r > home)
-        def _():
-            down(i, slot(i)).wait_recv()
-
-            @pl.when(has_up)
-            def _():
-                up(i, slot(i)).start()
-
-        @pl.when(r < home)
-        def _():
-            up(i, slot(i)).wait_recv()
-
-            @pl.when(has_down)
-            def _():
-                down(i, slot(i)).start()
+    pairs = mirror_pairs(n_rows)
+    targets = {q: [row for row, at in pairs if at == q] for q in range(n_rows)}
+    own = x_ref.at[:, pl.ds(pl.multiple_of(part * width, 128), width)]
+
+    def send(i, row):
+        return remote(own, tile, send_sems.at[i], recv_sem.at[0], row=row)
 
     @pl.when(now == 0)
     def _():
-        meet(n_rows, 0)
-
-        @pl.when(r == home)
-        def _():
-            for i in range(chunks):
-                own = x_ref.at[:, pl.ds(pl.multiple_of(part * width + i * step, 128), step)]
-
-                @pl.when(has_up)
+        barrier = pltpu.get_barrier_semaphore()
+        for q in range(n_rows):
+
+            @pl.when((r == q) & (home == q))
+            def _():
+                for row in targets[q]:
+                    greet(barrier, row=row)
+                if targets[q]:
+                    pl.semaphore_wait(barrier, len(targets[q]))
+                for i, row in enumerate(targets[q]):
+                    send(i, row).start()
+
+            for row in targets[q]:
+
+                @pl.when((r == row) & (home == q))
                 def _():
-                    up(i, own).start()
-
-                @pl.when(has_down)
-                def _():
-                    down(i, own).start()
+                    greet(barrier, row=q)
+                    pl.semaphore_wait(barrier, 1)
 
         high, low = halves(x_ref[...])
         x_parts[:m] = high
@@ -139,40 +135,29 @@
         def _():
             out_ref[at * m : (at + 1) * m] += value
 
-    for away in range(1, n_rows):
-        for i in range(per):
-            chunk = per * now + i - 2 * away
-
-            @pl.when(((r == home + away) | (r == home - away)) & (chunk >= 0) & (chunk < chunks))
-            def _():
-                relay(chunk)
-
     @pl.when(now == steps - 1)
     def _():
-        for away in range(1, n_rows):
-
-            @pl.when((r == home + away) | (r == home - away))
-            def _():
-                for i in range(max(chunks - 2 * away, 0), chunks):
-                    relay(i)
-
-        @pl.when((r >= home) & has_up)
-        def _():
-            for i in range(chunks):
-                up(i, slot(i)).wait_send()
-
-        @pl.when((r <= home) & has_down)
-        def _():
-            for i in range(chunks):
-                down(i, slot(i)).wait_send()
-
-        @pl.when(r == home)
-        def _():
-            tile_ref[...] = x_ref[:, pl.ds(pl.multiple_of(part * width, 128), width)]
-
-        @pl.when(r != home)
-        def _():
-            tile_ref[...] = tile[...]
+        for q in range(n_rows):
+
+            @pl.when((r == q) & (home == q))
+            def _():
+                for i, row in enumerate(targets[q]):
+                    send(i, row).wait_send()
+                tile_ref[...] = own[...]
+
+            for row in range(n_rows):
+                if row in targets[q]:
+
+                    @pl.when((r == row) & (home == q))
+                    def _():
+                        send(0, q).wait_recv()
+                        tile_ref[...] = 2.0 * tile[...]
+
+                elif row != q:
+
+                    @pl.when((r == row) & (home == q))
+                    def _():
+                        tile_ref[...] = jnp.zeros_like(tile_ref)
 
 
 TK, TN = 4096, 256
@@ -184,18 +169,16 @@
     cols = a_matrix.shape[1]
     tk, tn = min(TK, rows), min(TN, cols)
     grid = (cols // tn, rows // tk)
-    steps = grid[0] * grid[1]
-    chunks = max(steps, cols // 128)
     block = pl.BlockSpec((tk, tn), lambda n, k: (k, n))
     shape = lambda rows: jax.ShapeDtypeStruct((rows, cols), jnp.float32)
     return pl.pallas_call(
-        functools.partial(apply_kernel, n_rows, n_cols, chunks, steps),
+        functools.partial(apply_kernel, n_rows, n_cols, grid[0] * grid[1]),
         out_shape=(shape(2 * m), shape(m)),
         grid=grid,
         in_specs=[pl.BlockSpec(memory_space=pltpu.VMEM), block, block],
         out_specs=[pl.BlockSpec((2 * m, tn), lambda n, k: (0, n)), pl.BlockSpec(memory_space=pltpu.VMEM)],
         scratch_shapes=[pltpu.VMEM((2 * m, rows), jnp.bfloat16), pltpu.VMEM((m, cols), jnp.float32)]
-        + [pltpu.SemaphoreType.DMA((chunks,))] * 3,
+        + [pltpu.SemaphoreType.DMA((n_rows,)), pltpu.SemaphoreType.DMA((1,))],
         compiler_params=pltpu.CompilerParams(
             collective_id=collective_id, has_side_effects=True, dimension_semantics=("arbitrary", "arbitrary")
         ),
@@ -339,7 +322,7 @@
     n_rows, n_cols = lax.axis_size("row"), lax.axis_size("col")
     m, width = value.shape
     ratio = n_cols // n_rows
-    chunks = min(8, width // 128)
+    chunks = min(4, width // 128)
     dma = pltpu.SemaphoreType.DMA
     return pl.pallas_call(
         functools.partial(gather_kernel, n_rows, n_cols, chunks),
@@ -612,7 +595,10 @@
     w, mix, kept_a, kept_b = first_ritz(order, k, grams)
     resid = gather_sum(mm(mix, prods, 0, 0, HIGH), 2)
     fresh, resid_tile = apply_both(resid, a_matrix, b_matrix, 3)
-    grams = total(mm(fresh, jnp.concatenate([tile, resid_tile], axis=0), 1, 1, HIGH), 4)
+    ends = mm(fresh, tile, 1, 1, HIGH)
+    mirror = mm(resid_tile, prods, 1, 1, HIGH)
+    mirror = jnp.concatenate([mirror[:, : 3 * k], mirror[:, 3 * k :]], axis=0)
+    grams = total(jnp.concatenate([0.5 * (ends + mirror), mm(fresh, resid_tile, 1, 1, HIGH)], axis=1), 4)
     wide, inner, mix, mix_in = second_ritz(order, k, kept_a, kept_b, w, grams)
     last = gather_sum(mm(mix, prods, 0, 0, HIGH) + mm(mix_in, fresh, 0, 0, HIGH), 5)
     both = mm(wide, panel, 0, 0, HIGH) + mm(inner, resid, 0, 0, HIGH)

time: 258 us -> 241 us (0.934); the launches traced: 258 us -> 238 us
  Pallas kernels: 232 us -> 210 us
    pallas_call x2, Pallas kernels: 74.3 us -> 55.9 us  [apply_both(): pl.pallas_call(functools.partial(apply_kernel, n_rows, n_cols, grid[0] *...]
    pallas_call x2, Pallas kernels: 80.9 us -> 70 us  [gather_sum(): pl.pallas_call(functools.partial(gather_kernel, n_rows, n_cols, chunks),...]
    pallas_call x2, Pallas kernels: 44.2 us -> 51.1 us  [sum_over(): pl.pallas_call(functools.partial(sum_kernel, n_rows, n_cols, over_rows),...]
    dot_general x7 -> x9, matrix products: 18 us -> 19.9 us  [mm(): lax.dot_general(left, right, (((lc,), (rc,)), ((), ())), precision=precis...]
where the time goes in v3:
time: 241 us; the launch traced here: 238 us
  Pallas kernels  210 us (87%)
  matrix products  19.9 us (8%)
  other arithmetic  3.86 us (2%)
  local copies, waits for them, and re-layouts  3.36 us (1%)
    pallas_call x2, Pallas kernels, gather_sum(): pl.pallas_call(functools.partial(gather_kernel, n_rows, n_cols, chunks),...  70 us
    pallas_call x2, Pallas kernels, apply_both(): pl.pallas_call(functools.partial(apply_kernel, n_rows, n_cols, grid[0] *...  55.9 us
    pallas_call x2, Pallas kernels, sum_over(): pl.pallas_call(functools.partial(sum_kernel, n_rows, n_cols, over_rows),...  51.1 us
    pallas_call x2, Pallas kernels, in_vmem(): pl.pallas_call(kernel, out_shape=tuple((jax.ShapeDtypeStruct(dims, jnp.fl...  33 us
    dot_general x9, matrix products, mm(): lax.dot_general(left, right, (((lc,), (rc,)), ((), ())), precision=precis...  19.9 us

profile of v3, /device:TPU:13, one launch (start us, length us, event | category | flops | bytes accessed | tf_op | source)
XLA Modules:
  0.0 238.0 jit_solution(3996561946291970818)
XLA Ops:
  0.6 3.8 %pad_maximum_fusion.x_ref = f32[192,4096]{1,0:T(8,128)} fusion(f32[64,4096]{1,0:T(8,128)} %bitcast.28, f32[64,4096]{1,0:T(8,128)} %bitcast.30, f32[64,4096]{1,0:T(8,128)} %bitcast.32), kind=kLoop, calls=%fused_computation.1 | loop fusion | flops 1572864 | bytes 6291456 | tf_op jit(solution)/shard_map/concatenate | solution.py:592
  4.5 30.8 %apply_both.2 = (f32[384,2048]{1,0:T(8,128)}, f32[192,2048]{1,0:T(8,128)}) custom-call(f32[192,4096]{1,0:T(8,128)} %pad_maximum_fusion.x_ref, f32[4096,2048]{1,0:T(8,128)} %a_ref.3, f32[4096,2048]{1,0:T(8,128)} %b_ref.3), custom_call_target="tpu_custom_call" | custom-call | tf_op jit(solution)/shard_map/apply_both/pallas_call | solution.py:174
  35.3 0.0 copy-start
  35.3 4.7 %fusion.3 = f32[384,192]{1,0:T(8,128)} fusion(f32[384,2048]{1,0:T(8,128)} %get-tuple-element.15, f32[192,2048]{1,0:T(8,128)} %get-tuple-element.16), kind=kOutput, calls=%fused_computation.10 | convolution fusion | flops 905969664 | bytes 5013504 | tf_op jit(solution)/shard_map/dot_general | solution.py:18
  40.0 33.0 %sum_over.2.grams_ref = f32[8,48,192]{2,1,0:T(8,128)} custom-call(f32[8,48,192]{2,1,0:T(8,128)} %bitcast.34), custom_call_target="tpu_custom_call" | custom-call | tf_op jit(solution)/shard_map/sum_over/pallas_call | solution.py:421
  73.0 16.4 %first_ritz.1 = (f32[192,128]{1,0:T(8,128)}, f32[384,64]{1,0:T(8,128)}, f32[128,128]{1,0:T(8,128)}, f32[128,128]{1,0:T(8,128)}) custom-call(f32[8,48,192]{2,1,0:T(8,128)} %sum_over.2.grams_ref), custom_call_target="tpu_custom_call" | custom-call | tf_op jit(solution)/shard_map/first_ritz/pallas_call | solution.py:567
  89.3 0.0 copy-done
  89.3 2.8 %fusion.4.x_ref = f32[64,2048]{1,0:T(8,128)} fusion(f32[384,64]{1,0:T(8,128)} %get-tuple-element.20, f32[384,2048]{1,0:T(8,128)S(1)} %copy-done), kind=kOutput, calls=%fused_computation.11 | convolution fusion | flops 301989888 | bytes 3768320 | tf_op jit(solution)/shard_map/dot_general | solution.py:18
  92.1 35.2 %gather_sum.2.x_ref = f32[64,4096]{1,0:T(8,128)} custom-call(f32[64,2048]{1,0:T(8,128)} %fusion.4.x_ref), custom_call_target="tpu_custom_call" | custom-call | tf_op jit(solution)/shard_map/gather_sum/pallas_call | solution.py:327
  127.3 25.1 %apply_both.3 = (f32[128,2048]{1,0:T(8,128)}, f32[64,2048]{1,0:T(8,128)}) custom-call(f32[64,4096]{1,0:T(8,128)} %gather_sum.2.x_ref, f32[4096,2048]{1,0:T(8,128)} %a_ref.3, f32[4096,2048]{1,0:T(8,128)} %b_ref.3), custom_call_target="tpu_custom_call" | custom-call | tf_op jit(solution)/shard_map/apply_both/pallas_call | solution.py:174
  152.4 0.0 copy-start.2
  152.4 0.0 copy-start.4
  152.4 2.2 fusion.6
  154.6 2.4 %fusion.5 = f32[64,384]{0,1:T(8,128)S(1)} fusion(f32[64,2048]{1,0:T(8,128)} %get-tuple-element.22, f32[384,2048]{1,0:T(8,128)S(1)} %copy-done), kind=kOutput, calls=%fused_computation.12 | convolution fusion | flops 301989888 | bytes 3768320 | tf_op jit(solution)/shard_map/dot_general | solution.py:18
  157.1 0.0 copy-done.2
  157.1 0.0 copy-done.4
  157.1 0.8 fusion
  157.9 0.8 copy.11
  158.7 18.2 %sum_over.3.grams_ref = f32[8,16,256]{2,1,0:T(8,128)} custom-call(f32[8,16,256]{2,1,0:T(8,128)} %bitcast.35), custom_call_target="tpu_custom_call" | custom-call | tf_op jit(solution)/shard_map/sum_over/pallas_call | solution.py:421
  176.9 16.7 %second_ritz.1 = (f32[192,128]{1,0:T(8,128)}, f32[64,128]{1,0:T(8,128)}, f32[384,64]{1,0:T(8,128)}, f32[128,64]{1,0:T(8,128)}) custom-call(f32[128,128]{1,0:T(8,128)} %get-tuple-element.17.wa_ref, f32[128,128]{1,0:T(8,128)} %get-tuple-element.18.wb_ref, f32[192,128]{1,0:T(8,128)} %get-tuple-element.19.w_ref, f32[8,16,256]{2,1,0:T(8,128)} %sum_over.3.grams_ref), custom_call_target="tpu_custom_call" | custom-call | tf_op jit(solution)/shard_map/second_ritz/pallas_call | solution.py:567
  193.5 0.0 copy-start.3
  193.5 0.0 copy-start.9
  193.5 0.0 copy-start.8
  193.5 2.3 fusion.7
  195.9 0.0 copy-done.3
  195.9 0.0 copy-done.9
  195.9 0.0 copy-start.6
  195.9 0.0 copy-start.7
  195.9 1.3 convolution_add_fusion.1.x_ref
  197.2 0.0 copy-start.1
  197.2 0.0 copy-start.10
  197.2 34.7 %gather_sum.3 = f32[64,4096]{1,0:T(8,128)} custom-call(f32[64,2048]{1,0:T(8,128)} %convolution_add_fusion.1.x_ref), custom_call_target="tpu_custom_call" | custom-call | tf_op jit(solution)/shard_map/gather_sum/pallas_call | solution.py:327
  232.0 0.0 copy-done.8
  232.0 0.0 copy-done.6
  232.0 0.0 copy-done.7
  232.0 2.3 fusion.1
  234.3 0.0 copy-done.1
  234.3 0.0 copy-done.10
  234.3 1.1 convolution_add_fusion
  235.4 0.0 copy-start.5
  235.4 1.5 slice_bitcast_fusion
  236.9 0.1 copy-done.5
  237.0 1.0 copy.15
  (2 shorter events, 0.0 us)
Async XLA Ops:
  35.3 54.0 %copy-start = (f32[384,2048]{1,0:T(8,128)S(1)}, f32[384,2048]{1,0:T(8,128)}, u32[]{:S(2)}) copy-start(f32[384,2048]{1,0:T(8,128)} %get-tuple-element.15) | copy-start | bytes 9437188
  152.4 4.6 %copy-start.2 = (f32[128,2048]{1,0:T(8,128)S(1)}, f32[128,2048]{1,0:T(8,128)}, u32[]{:S(2)}) copy-start(f32[128,2048]{1,0:T(8,128)} %get-tuple-element.21) | copy-start | bytes 3145732
  152.4 4.6 %copy-start.4 = (f32[192,2048]{1,0:T(8,128)S(1)}, f32[192,2048]{1,0:T(8,128)}, u32[]{:S(2)}) copy-start(f32[192,2048]{1,0:T(8,128)} %get-tuple-element.16) | copy-start | bytes 4718596
  193.5 2.4 copy-start.3
  193.5 2.4 copy-start.9
  193.5 38.4 %copy-start.8 = (f32[192,128]{1,0:T(8,128)S(1)}, f32[192,128]{1,0:T(8,128)}, u32[]{:S(2)}) copy-start(f32[192,128]{1,0:T(8,128)} %get-tuple-element.23) | copy-start | bytes 294916
  195.9 36.1 %copy-start.6 = (f32[4096,64]{0,1:T(8,128)S(1)}, f32[4096,64]{0,1:T(8,128)}, u32[]{:S(2)}) copy-start(f32[4096,64]{0,1:T(8,128)} %param.9) | copy-start | bytes 3145732
  195.9 36.1 %copy-start.7 = (f32[4096,64]{0,1:T(8,128)S(1)}, f32[4096,64]{0,1:T(8,128)}, u32[]{:S(2)}) copy-start(f32[4096,64]{0,1:T(8,128)} %param.8) | copy-start | bytes 3145732
  197.2 37.1 %copy-start.1 = (f32[64,4096]{1,0:T(8,128)S(1)}, f32[64,4096]{1,0:T(8,128)}, u32[]{:S(2)}) copy-start(f32[64,4096]{1,0:T(8,128)} %gather_sum.2.x_ref) | copy-start | bytes 3145732
  197.2 37.1 %copy-start.10 = (f32[64,128]{1,0:T(8,128)S(1)}, f32[64,128]{1,0:T(8,128)}, u32[]{:S(2)}) copy-start(f32[64,128]{1,0:T(8,128)} %get-tuple-element.24) | copy-start | bytes 98308
  235.4 1.6 copy-start.5
